TPU v7x, 16 devices: a whole 2x2x2 slice. The times are simulated.
16 devices in a mesh: dp: 1, ep: 16 (over x, y, z, core).
Axes of the slice: x: 2, y: 2, z: 2, core: 2. Of those that a mesh axis runs over, the one named last changes fastest.
Arguments:
- x: bfloat16 [1, 16, 256, 2560], P('dp', 'ep')
- expert: int32 [1, 16, 256, 8], P('dp', 'ep')
- slot: int32 [1, 16, 256, 8], P('dp', 'ep')
- gate: float32 [1, 16, 256, 8], P('dp', 'ep')
- w_gate: bfloat16 [80, 2560, 1536], P('ep')
- w_up: bfloat16 [80, 2560, 1536], P('ep')
- w_down: bfloat16 [80, 1536, 2560], P('ep')
- s_gate: bfloat16 [2560, 1536], replicated
- s_up: bfloat16 [2560, 1536], replicated
- s_down: bfloat16 [1536, 2560], replicated
Outputs:
- y: bfloat16 [1, 16, 256, 2560], P('dp', 'ep')
All inputs are finite; a program needn't handle non-finite values.
Results may differ from a plain program's by a relative error of at most 0.009.
Values are sent between devices in bfloat16 or wider.
A program may use at most 2 GiB of HBM per device.

v0:
```python
import jax
import jax.numpy as jnp
from jax import lax
from jax.sharding import NamedSharding, PartitionSpec as P


def einsum(form, a, b):
    return jnp.einsum(form, a.astype(jnp.float32), b.astype(jnp.float32))


def for_all(x, s_gate, s_up, s_down):
    h = jax.nn.silu(einsum("...d,df->...f", x, s_gate)) * einsum("...d,df->...f", x, s_up)
    return einsum("...f,fd->...d", h.astype(jnp.bfloat16), s_down)


def solution(mesh):
    def placed(v, *spec):
        return lax.with_sharding_constraint(v, NamedSharding(mesh, P(*spec)))

    def step(x, expert, slot, gate, w_gate, w_up, w_down, s_gate, s_up, s_down):
        experts, (tokens, top) = w_gate.shape[0], expert.shape[2:]
        slots = 5 * tokens * top // (4 * experts)
        to_expert = jax.nn.one_hot(expert, experts, dtype=jnp.bfloat16)
        to_slot = jax.nn.one_hot(slot, slots, dtype=jnp.bfloat16)
        weighted = to_expert * gate[..., None].astype(jnp.bfloat16)
        dispatch = einsum("abtke,abtkc->abtec", to_expert, to_slot).astype(jnp.bfloat16)
        combine = einsum("abtke,abtkc->abtec", weighted, to_slot).astype(jnp.bfloat16)
        z = einsum("abtec,abtd->aebcd", dispatch, x).astype(jnp.bfloat16)
        z = placed(z, "dp", None, "ep", None, None)
        z = placed(z, "dp", "ep", None, None, None)
        h = jax.nn.silu(einsum("aebcd,edf->aebcf", z, w_gate))
        h = (h * einsum("aebcd,edf->aebcf", z, w_up)).astype(jnp.bfloat16)
        out = einsum("aebcf,efd->aebcd", h, w_down).astype(jnp.bfloat16)
        out = placed(out, "dp", "ep", None, None, None)
        out = placed(out, "dp", None, "ep", None, None)
        y = einsum("abtec,aebcd->abtd", combine, out)
        return (y + for_all(x, s_gate, s_up, s_down)).astype(jnp.bfloat16)

    return step
```

profile of v0, /device:TPU:0, one launch (start us, length us, event | category | flops | bytes accessed | tf_op | source)
XLA Modules:
  0.0 486.4 jit_solution(1711438075584884766)
XLA Ops:
  0.0 0.0 copy-start
  0.0 0.9 copy.10
  0.9 0.0 copy-start.1
  0.9 1.5 copy.12
  2.5 3.6 convolution_convert_fusion.2
  6.1 3.0 copy.13
  9.1 0.0 copy-done
  9.1 5.1 %convolution_convert_fusion = bf16[80,32,2560]{2,1,0:T(8,128)(2,1)S(1)} fusion(bf16[256,80,32]{0,2,1:T(8,128)(2,1)} %copy.13, bf16[1,1,256,2560]{3,2,1,0:T(8,128)(2,1)S(1)} %copy-done), kind=kOutput, calls=%fused_computation.18 | convolution fusion | flops 3361996800 | bytes 15728640 | tf_op jit(solution)/abtec,abtd->aebcd/dot_general | solution.py:8
  14.2 0.0 copy-done.1
  14.2 150.5 %all-to-all.4 = bf16[1,16,5,1,32,2560]{5,4,2,3,0,1:T(8,128)(2,1)} all-to-all(bf16[1,16,5,1,32,2560]{5,4,2,3,0,1:T(8,128)(2,1)S(1)} %bitcast.139), channel_id=1, replica_groups=mesh['dp'=1,'ep'=16] {'ep'}, dimensions={1} | all-to-all | bytes 26214400 | tf_op jit(solution)/sharding_constraint;jit(solution)/sharding_constraint | solution.py:18
  164.7 30.1 %fusion.2 = f32[5,16,32,1536]{3,2,1,0:T(8,128)} fusion(bf16[5,2560,1536]{2,1,0:T(8,128)(2,1)} %param.5, bf16[1,16,5,1,32,2560]{5,4,2,3,0,1:T(8,128)(2,1)} %all-to-all.4), kind=kOutput, calls=%fused_computation.2 | convolution fusion | flops 20132659200 | bytes 68157440 | tf_op jit(solution)/aebcd,edf->aebcf/dot_general | solution.py:8
  194.8 30.2 %fusion.4 = f32[5,16,32,1536]{3,2,1,0:T(8,128)} fusion(bf16[5,2560,1536]{2,1,0:T(8,128)(2,1)} %param.4, bf16[1,16,5,1,32,2560]{5,4,2,3,0,1:T(8,128)(2,1)} %all-to-all.4), kind=kOutput, calls=%fused_computation.4 | convolution fusion | flops 20132659200 | bytes 68157440 | tf_op jit(solution)/aebcd,edf->aebcf/dot_general | solution.py:8
  225.0 28.2 %convert_bitcast_fusion = bf16[1,5,16,1,32,2560]{5,4,2,1,3,0:T(8,128)(2,1)S(1)} fusion(bf16[5,1536,2560]{2,1,0:T(8,128)(2,1)} %param.6, f32[5,16,32,1536]{3,2,1,0:T(8,128)} %fusion.2, f32[5,16,32,1536]{3,2,1,0:T(8,128)} %fusion.4), kind=kOutput, calls=%fused_computation.15 | convolution fusion | flops 20162805760 | bytes 83886080 | tf_op jit(solution)/aebcf,efd->aebcd/dot_general | solution.py:8
  253.2 6.5 %copy.16 = bf16[1,5,16,1,32,2560]{5,4,1,3,0,2:T(8,128)(2,1)} copy(bf16[1,5,16,1,32,2560]{5,4,2,1,3,0:T(8,128)(2,1)S(1)} %convert_bitcast_fusion) | data formatting | bytes 26214400 | tf_op jit(solution)/sharding_constraint;jit(solution)/sharding_constraint | solution.py:18
  259.7 0.0 copy-start.4
  259.7 0.0 copy-start.2
  259.7 0.0 copy-start.3
  259.7 4.0 all-to-all-start.1
  263.8 0.0 copy-done.4
  263.8 0.1 copy.11
  263.9 0.0 copy-done.2
  263.9 0.0 copy-done.3
  263.9 4.0 convolution_convert_fusion.1
  267.9 3.6 copy.23
  271.5 6.6 %convolution_bitcast_fusion.2 = f32[1,256,1536]{2,1,0:T(8,128)} fusion(bf16[2560,1536]{1,0:T(8,128)(2,1)} %param.7, bf16[1,1,256,2560]{3,2,1,0:T(8,128)(2,1)S(1)} %copy-done), kind=kOutput, calls=%fused_computation.26 | convolution fusion | flops 2013265920 | bytes 10747904 | tf_op jit(solution)/...d,df->...f/dot_general | solution.py:8
  278.2 11.7 %fusion.34 = f32[256,2560]{1,0:T(8,128)} fusion(bf16[1536,2560]{1,0:T(8,128)(2,1)} %param.9, bf16[2560,1536]{1,0:T(8,128)(2,1)} %param.8, f32[1,256,1536]{2,1,0:T(8,128)} %convolution_bitcast_fusion.2, bf16[1,1,256,2560]{3,2,1,0:T(8,128)(2,1)S(1)} %copy-done), kind=kOutput, calls=%fused_computation.39 | convolution fusion | flops 4028891136 | bytes 21233664 | tf_op jit(solution)/...f,fd->...d/dot_general | solution.py:8
  289.9 186.8 %all-to-all-done.1 = bf16[1,5,16,1,32,2560]{5,4,1,3,0,2:T(8,128)(2,1)} async-done(((bf16[1,5,16,1,32,2560]{5,4,1,3,0,2:T(8,128)(2,1)}), bf16[1,5,16,1,32,2560]{5,4,1,3,0,2:T(8,128)(2,1)}, u32[]{:S(2)}, u32[]{:S(2)}) %all-to-all-start.1) | async-done | bytes 13107232 | tf_op jit(solution)/sharding_constraint;jit(solution)/sharding_constraint | solution.py:18
  476.6 9.8 %fusion.20 = bf16[1,1,256,2560]{3,2,1,0:T(8,128)(2,1)} fusion(f32[256,2560]{1,0:T(8,128)} %fusion.34, bf16[256,80,32]{0,2,1:T(8,128)(2,1)S(1)} %copy.23, bf16[80,32,2560]{2,1,0:T(8,128)(2,1)} %bitcast.38), kind=kOutput, calls=%fused_computation.23 | convolution fusion | flops 3356753920 | bytes 18350080 | tf_op jit(solution)/abtec,aebcd->abtd/dot_general | solution.py:8
  (1 shorter events, 0.0 us)
Async XLA Ops:
  0.0 9.1 %copy-start = (bf16[1,1,256,2560]{3,2,1,0:T(8,128)(2,1)S(1)}, bf16[1,1,256,2560]{3,2,1,0:T(8,128)(2,1)}, u32[]{:S(2)}) copy-start(bf16[1,1,256,2560]{3,2,1,0:T(8,128)(2,1)} %param.3) | copy-start | bytes 3932164
  0.9 13.3 %copy-start.1 = (s32[256,8]{1,0:T(8,128)}, s32[256,8]{1,0:T(8,128)S(1)}, u32[]{:S(2)}) copy-start(s32[256,8]{1,0:T(8,128)S(1)} %copy.10) | copy-start | bytes 24580
  259.7 4.0 copy-start.4
  259.7 4.2 copy-start.2
  259.7 4.2 copy-start.3
  259.7 216.9 %all-to-all-start.1 = ((bf16[1,5,16,1,32,2560]{5,4,1,3,0,2:T(8,128)(2,1)}), bf16[1,5,16,1,32,2560]{5,4,1,3,0,2:T(8,128)(2,1)}, u32[]{:S(2)}, u32[]{:S(2)}) async-start(bf16[1,5,16,1,32,2560]{5,4,1,3,0,2:T(8,128)(2,1)} %copy.16), calls=%async_computation.1 | async-start | bytes 26214400 | tf_op jit(solution)/sharding_constraint;jit(solution)/sharding_constraint | solution.py:18
where the time goes:
time: 487 us; the launch traced here: 486 us
  waiting for transfers between devices  187 us (38%)
  blocking collectives  151 us (31%)
  matrix products  129 us (26%)
  local copies, waits for them, and re-layouts  15.7 us (3%)
    another operation x1, waiting for transfers between devices, placed(): return lax.with_sharding_constraint(v, NamedSharding(mesh, P(*spec)))  187 us
    another operation x1, blocking collectives, placed(): return lax.with_sharding_constraint(v, NamedSharding(mesh, P(*spec)))  151 us
    dot_general x9, matrix products, einsum(): return jnp.einsum(form, a.astype(jnp.float32), b.astype(jnp.float32))  129 us
  transfers between devices with their start and end apart: 1, of which 1 were waited for; matrix products, arithmetic and copies ran while one was open for 5% of the time, Pallas kernels for 0%

commit v1 on v0

v1 whole, which is shorter than its diff:
```python
import functools

import jax
import jax.numpy as jnp
from jax import lax
from jax.experimental import pallas as pl
from jax.experimental.pallas import tpu as pltpu
from jax.sharding import PartitionSpec as P

MESH = pl.DeviceIdType.MESH
F32, BF16 = jnp.float32, jnp.bfloat16
ROWS = ((0, 96), (96, 80), (176, 80))
KU, KW = 5, 512
NU, NW = 10, 256
NE, CAP = 5, 32
RING = 5
PRE = 4
HB = 40


def kernel(meta_ref, x_ref, wg_ref, wu_ref, wd_ref, sg_ref, su_ref, sd_ref, y_ref,
           gmeta, onehot, comb, xg, acc, z, wgu, wdn, ys, ob, rc, rb, ra, sc, sb, sa, yst,
           m_send, m_recv, ag_a, ag_b, ag_c, ag_p, ag_s, ag_ps, free,
           gu_sem, dn_sem, o_recv, o_send, o_free, c_recv, b_recv, a_recv, c_send, b_send, a_send, y_sem):
    me = lax.axis_index("ep")
    core = me % 2
    chip = me // 2
    partner = me + 1 - 2 * core
    dx = 4 * (1 - 2 * ((chip // 4) % 2))
    dy = 2 * (1 - 2 * ((chip // 2) % 2))
    dz = 1 - 2 * (chip % 2)

    def delta(t):
        return dx + t * (dy - dx) + ((t * (t - 1)) // 2) * (dz - 2 * dy + dx)

    def order(i, u):
        return delta((i + u) % 3), delta((i + u + 1) % 3), delta((i + u + 2) % 3)

    def peer(d):
        return 2 * (chip + d) + core

    def remote(src, dst, send, recv, dev):
        return pltpu.make_async_remote_copy(
            src_ref=src, dst_ref=dst, send_sem=send, recv_sem=recv, device_id={"ep": dev}, device_id_type=MESH)

    def start_gu(i):
        slot = i % 2

        @pl.when(i < KU)
        def _():
            rows = pl.ds(pl.multiple_of(i * KW, KW), KW)
            pltpu.make_async_copy(sg_ref.at[rows], wgu.at[slot, 0], gu_sem.at[slot, 0]).start()
            pltpu.make_async_copy(su_ref.at[rows], wgu.at[slot, 1], gu_sem.at[slot, 1]).start()

        @pl.when(jnp.logical_and(i >= KU, i < KU + 2 * KU * NE))
        def _():
            m = (i - KU) % (KU * NE)
            rows = pl.ds(pl.multiple_of((m // NE) * KW, KW), KW)
            pltpu.make_async_copy(wg_ref.at[m % NE, rows], wgu.at[slot, 0], gu_sem.at[slot, 0]).start()
            pltpu.make_async_copy(wu_ref.at[m % NE, rows], wgu.at[slot, 1], gu_sem.at[slot, 1]).start()

    def wait_gu(i):
        slot = i % 2
        for j in range(2):
            pltpu.make_async_copy(sg_ref.at[pl.ds(0, KW)], wgu.at[slot, j], gu_sem.at[slot, j]).wait()

    def start_dn(i):
        slot = i % 3

        @pl.when(i < NU)
        def _():
            cols = pl.ds(pl.multiple_of(i * NW, NW), NW)
            pltpu.make_async_copy(sd_ref.at[:, cols], wdn.at[slot], dn_sem.at[slot]).start()

        @pl.when(jnp.logical_and(i >= NU, i < NU + 2 * NU * NE))
        def _():
            m = i - NU
            cols = pl.ds(pl.multiple_of(((m // NE) % NU) * NW, NW), NW)
            pltpu.make_async_copy(wd_ref.at[m % NE, :, cols], wdn.at[slot], dn_sem.at[slot]).start()

    def wait_dn(i):
        slot = i % 3
        pltpu.make_async_copy(sd_ref.at[:, pl.ds(0, NW)], wdn.at[slot], dn_sem.at[slot]).wait()

    def blk(k, s):
        return k * 8 + s

    def own(q):
        k = q % KU
        cols = pl.ds(pl.multiple_of(k * KW, KW), KW)

        @pl.when(q >= KU)
        def _():
            pl.semaphore_wait(free.at[k], 4)

        for stage, sem in enumerate((ag_a, ag_b, ag_c)):
            for i, (r0, rn) in enumerate(ROWS):
                d = order(i, k)[stage]
                remote(x_ref.at[pl.ds(r0, rn), cols], xg.at[blk(k, chip), pl.ds(r0, rn)],
                       ag_s.at[k], sem.at[k], peer(d)).start()
        remote(x_ref.at[:, cols], xg.at[blk(k, chip)], ag_ps.at[k], ag_p.at[k], partner).start()
        xg[blk(k, chip)] = x_ref[:, cols]

    def arrived(sem, k, n):
        remote(xg.at[pl.ds(0, n)], xg.at[pl.ds(0, n)], ag_s.at[k], sem.at[k], partner).wait_recv()

    def forward(b, r0, rn, k, sem, dev):
        part = xg.at[b, pl.ds(r0, rn)]
        remote(part, part, ag_s.at[k], sem.at[k], dev).start()

    def forward_p(b, r0, rn, k):
        part = xg.at[b, pl.ds(r0, rn)]
        remote(part, part, ag_ps.at[k], ag_p.at[k], partner).start()

    def event_a(k):
        arrived(ag_a, k, 1)
        for i, (r0, rn) in enumerate(ROWS):
            a, b, c = order(i, k)
            forward(blk(k, chip + a), r0, rn, k, ag_b, peer(b))
        for i, (r0, rn) in enumerate(ROWS):
            a, b, c = order(i, k)
            forward(blk(k, chip + a), r0, rn, k, ag_c, peer(c))
        for i, (r0, rn) in enumerate(ROWS):
            a, b, c = order(i, k)
            forward_p(blk(k, chip + a), r0, rn, k)

    def event_b(k):
        arrived(ag_b, k, 2)
        for i, (r0, rn) in enumerate(ROWS):
            a, b, c = order(i, k)
            forward(blk(k, chip + b), r0, rn, k, ag_c, peer(c))
            forward(blk(k, chip + b + a), r0, rn, k, ag_c, peer(c))
        for i, (r0, rn) in enumerate(ROWS):
            a, b, c = order(i, k)
            forward_p(blk(k, chip + b), r0, rn, k)
            forward_p(blk(k, chip + b + a), r0, rn, k)

    def event_c(k):
        arrived(ag_c, k, 4)
        for i, (r0, rn) in enumerate(ROWS):
            a, b, c = order(i, k)
            for d in (c, c + a, c + b, c + b + a):
                forward_p(blk(k, chip + d), r0, rn, k)

    def sent(k):
        remote(xg.at[pl.ds(0, 7)], xg.at[pl.ds(0, 7)], ag_s.at[k], ag_a.at[k], partner).wait_send()
        remote(xg.at[pl.ds(0, 8)], xg.at[pl.ds(0, 8)], ag_ps.at[k], ag_p.at[k], partner).wait_send()

    def act(n, store):
        def body(t, _):
            e, r = t // 8, t % 8
            rows = pl.ds(pl.multiple_of(r * 32, 32), 32)
            for q in range(3):
                cols = slice(q * KW, (q + 1) * KW)
                g = acc[e, 0, rows, cols]
                u = acc[e, 1, rows, cols]
                acc[e, 0, rows, cols] = jnp.zeros((32, KW), F32)
                acc[e, 1, rows, cols] = jnp.zeros((32, KW), F32)
                store(e, q, rows, (g * (1.0 / (1.0 + jnp.exp(-g))) * u).astype(BF16))
            return 0

        lax.fori_loop(0, n * 8, body, 0)

    def gate_up(i, lhs, e):
        wait_gu(i)
        slot = i % 2
        for j in range(2):
            acc[e, j] += jnp.dot(lhs, wgu[slot, j], preferred_element_type=F32)
        start_gu(i + 2)

    for i in range(2):
        start_gu(jnp.int32(i))
    for i in range(3):
        start_dn(jnp.int32(i))
    barrier = pltpu.get_barrier_semaphore()

    def greet(i, _):
        pl.semaphore_signal(barrier, inc=1, device_id={"ep": (me + i) % 16}, device_id_type=MESH)
        return 0

    lax.fori_loop(1, 16, greet, 0)
    pl.semaphore_wait(barrier, 15)

    @pl.when(core == 0)
    def _():
        own(jnp.int32(0))

    def tell(i, _):
        remote(meta_ref, gmeta.at[me], m_send, m_recv, (me + i) % 16).start()
        return 0

    lax.fori_loop(1, 16, tell, 0)
    gmeta[me] = meta_ref[...]

    @pl.when(core == 0)
    def _():
        own(jnp.int32(1))

    def clear(t, _):
        e, r = t // 8, t % 8
        rows = pl.ds(pl.multiple_of(r * 32, 32), 32)
        for j in range(2):
            acc[e, j, rows] = jnp.zeros((32, 1536), F32)
        return 0

    lax.fori_loop(0, NE * 8, clear, 0)

    def shared(i, _):
        @pl.when(jnp.logical_and(core == 0, i == 1))
        def _():
            event_a(jnp.int32(0))

        @pl.when(jnp.logical_and(core == 0, i == 4))
        def _():
            event_b(jnp.int32(0))

        gate_up(i, x_ref[:, pl.ds(pl.multiple_of(i * KW, KW), KW)], 0)
        return 0

    lax.fori_loop(0, KU, shared, 0)

    def store_shared(e, q, rows, v):
        z[q, rows] = v

    act(1, store_shared)

    def shared_down(i, _):
        wait_dn(i)
        slot = i % 3
        ys[i] = sum(jnp.dot(z[q], wdn[slot, q * KW:(q + 1) * KW], preferred_element_type=F32) for q in range(3))
        start_dn(i + 3)
        return 0

    lax.fori_loop(0, NU, shared_down, 0)

    remote(gmeta.at[pl.ds(0, 15)], gmeta.at[pl.ds(0, 15)], m_send, m_recv, partner).wait()

    def build_comb(s, _):
        m = gmeta[2 * s + core]
        row = lax.broadcasted_iota(jnp.int32, (384, 256), 0)
        mine = (me * (NE * CAP)).astype(jnp.int32)
        theirs = (partner * (NE * CAP)).astype(jnp.int32)
        target = jnp.where(row < 160, row + mine, jnp.where(row < 320, row - 160 + theirs, -7)).astype(F32)
        t = jnp.zeros((384, 256), F32)
        for j in range(8):
            t = t + jnp.where(target == m[j:j + 1], m[8 + j:9 + j], 0.0)
        comb[s] = t.T.astype(BF16)
        return 0

    lax.fori_loop(0, 8, build_comb, 0)

    def gather_step(g):
        ph, k = g // KU, g % KU
        nxt = g + 1

        @pl.when(core == ph)
        def _():
            event_c(k)

        @pl.when(core != ph)
        def _():
            arrived(ag_p, k, 8)

        @pl.when(jnp.logical_and(nxt < 2 * KU, core == nxt // KU))
        def _():
            event_a(nxt % KU)

        @pl.when(k == 0)
        def _():
            def build(s, _):
                m = gmeta[2 * s + ph]
                target = (lax.broadcasted_iota(jnp.int32, (160, 256), 0) + me * (NE * CAP)).astype(F32)
                t = jnp.zeros((160, 256), F32)
                for j in range(8):
                    t = jnp.where(target == m[j:j + 1], 1.0, t)
                onehot[s] = t.astype(BF16)
                return 0

            lax.fori_loop(0, 8, build, 0)

        for s in range(8):
            zs = jnp.dot(onehot[s], xg[blk(k, s)], preferred_element_type=F32).astype(BF16)
            for e in range(NE):
                z[e, s * CAP:(s + 1) * CAP] = zs[e * CAP:(e + 1) * CAP]

        def expert(e, _):
            @pl.when(e == 2)
            def _():
                @pl.when(jnp.logical_and(nxt < 2 * KU, core == nxt // KU))
                def _():
                    event_b(nxt % KU)

                @pl.when(jnp.logical_and(g + 2 < 2 * KU, core == (g + 2) // KU))
                def _():
                    own(g + 2)

            gate_up(KU + g * NE + e, z[e], e)
            return 0

        lax.fori_loop(0, NE, expert, 0)

        @pl.when(jnp.logical_and(ph == 0, core == 0))
        def _():
            sent(k)
            pl.semaphore_signal(free.at[k], inc=1, device_id={"ep": partner}, device_id_type=MESH)

        @pl.when(jnp.logical_and(ph == 0, core == 1))
        def _():
            for d in (dx, dy, dz):
                pl.semaphore_signal(free.at[k], inc=1, device_id={"ep": peer(d)}, device_id_type=MESH)

        @pl.when(k == KU - 1)
        def _():
            @pl.when(jnp.logical_and(ph == 1, core == 1))
            def _():
                for kk in range(KU):
                    sent(kk)

            def store(e, q, rows, v):
                xg[HB * (1 - ph) + e * 3 + q, rows] = v

            act(NE, store)

    def term(slot, d, r0, rn):
        return jnp.dot(comb[d, r0:r0 + rn, :320], ob[slot, d], preferred_element_type=F32)

    def sum_step(r):
        def main(v):
            return jnp.logical_and(jnp.logical_and(v >= 0, v < 2 * NU), core == v // NU)

        v4 = r - 5

        @pl.when(main(v4))
        def _():
            u, slot, p = v4 % NU, v4 % RING, v4 % 2
            remote(ra.at[u], ra.at[u], a_send.at[0], a_recv.at[u], partner).wait_recv()
            val = term(slot, chip, 0, 256) + rc[u, 0].astype(F32) + rb[u, 0].astype(F32) + ra[u].astype(F32) + ys[u]

            @pl.when(u >= 2)
            def _():
                pltpu.make_async_copy(yst.at[p], y_ref.at[:, pl.ds(0, NW)], y_sem.at[p]).wait()

            yst[p] = val.astype(BF16)
            cols = pl.ds(pl.multiple_of(u * NW, NW), NW)
            pltpu.make_async_copy(yst.at[p], y_ref.at[:, cols], y_sem.at[p]).start()

            @pl.when(u < NU - RING)
            def _():
                pl.semaphore_signal(o_free, inc=1, device_id={"ep": partner}, device_id_type=MESH)

        v3 = r - 4

        @pl.when(main(v3))
        def _():
            u, slot, p = v3 % NU, v3 % RING, v3 % 2
            remote(rb.at[u], rb.at[u], b_send.at[0], b_recv.at[u], partner).wait_recv()

            @pl.when(u >= 2)
            def _():
                remote(sa.at[p], sa.at[p], a_send.at[p], a_recv.at[0], partner).wait_send()

            for i, (r0, rn) in enumerate(ROWS):
                a, b, c = order(i, u)
                rows = slice(r0, r0 + rn)
                val = term(slot, chip + a, r0, rn) + rc[u, 1, rows].astype(F32) + rb[u, 1, rows].astype(F32)
                sa[p, rows] = val.astype(BF16)
            for i, (r0, rn) in enumerate(ROWS):
                a, b, c = order(i, u)
                remote(sa.at[p, pl.ds(r0, rn)], ra.at[u, pl.ds(r0, rn)], a_send.at[p], a_recv.at[u], peer(a)).start()

        v2 = r - 3

        @pl.when(main(v2))
        def _():
            u, slot, p = v2 % NU, v2 % RING, v2 % 2
            remote(rc.at[u], rc.at[u], c_send.at[0], c_recv.at[u], partner).wait_recv()

            @pl.when(u >= 2)
            def _():
                remote(sb.at[p], sb.at[p], b_send.at[p], b_recv.at[0], partner).wait_send()

            for i, (r0, rn) in enumerate(ROWS):
                a, b, c = order(i, u)
                rows = slice(r0, r0 + rn)
                for h in range(2):
                    val = term(slot, chip + b + h * a, r0, rn) + rc[u, 2 + h, rows].astype(F32)
                    sb[p, h, rows] = val.astype(BF16)
            for i, (r0, rn) in enumerate(ROWS):
                a, b, c = order(i, u)
                remote(sb.at[p, :, pl.ds(r0, rn)], rb.at[u, :, pl.ds(r0, rn)], b_send.at[p], b_recv.at[u],
                       peer(b)).start()

        @pl.when(r < 2 * NU)
        def _():
            ph, slot = r // NU, r % RING

            for e in range(NE):
                i = NU + r * NE + e
                wait_dn(i)
                o = sum(jnp.dot(xg[HB * (1 - ph) + e * 3 + q], wdn[i % 3, q * KW:(q + 1) * KW],
                                preferred_element_type=F32) for q in range(3)).astype(BF16)
                for s in range(8):
                    ob[slot, s, e * CAP:(e + 1) * CAP] = o[s * CAP:(s + 1) * CAP]
                start_dn(i + 3)

            @pl.when(core != ph)
            def _():
                @pl.when(r % NU >= RING)
                def _():
                    pl.semaphore_wait(o_free, 1)

                remote(ob.at[slot, :, pl.ds(0, 160)], ob.at[slot, :, pl.ds(160, 160)], o_send.at[slot],
                       o_recv.at[slot], partner).start()

        v1 = r - 1

        @pl.when(main(v1))
        def _():
            u, slot, p = v1 % NU, v1 % RING, v1 % 2
            part = ob.at[slot, :, pl.ds(160, 160)]
            remote(part, part, o_send.at[slot], o_recv.at[slot], partner).wait_recv()

            @pl.when(u >= 2)
            def _():
                remote(sc.at[p], sc.at[p], c_send.at[p], c_recv.at[0], partner).wait_send()

            for i, (r0, rn) in enumerate(ROWS):
                a, b, c = order(i, u)
                rows = slice(r0, r0 + rn)
                for h in range(4):
                    val = term(slot, chip + c + (h // 2) * b + (h % 2) * a, r0, rn)
                    sc[p, h, rows] = val.astype(BF16)
            for i, (r0, rn) in enumerate(ROWS):
                a, b, c = order(i, u)
                remote(sc.at[p, :, pl.ds(r0, rn)], rc.at[u, :, pl.ds(r0, rn)], c_send.at[p], c_recv.at[u],
                       peer(c)).start()

    def drained(r):
        v = r - RING

        @pl.when(jnp.logical_and(v >= 0, core != v // NU))
        def _():
            slot = v % RING
            part = ob.at[slot, :, pl.ds(0, 160)]
            remote(part, part, o_send.at[slot], o_recv.at[slot], partner).wait_send()

    def step(m, _):
        gather = jnp.logical_or(m < 2 * KU - 1, m == 2 * KU - 1 + PRE)

        @pl.when(gather)
        def _():
            gather_step(m - PRE * (m // (2 * KU - 1)))

        @pl.when(jnp.logical_not(gather))
        def _():
            r = m - (2 * KU - 1) - (m >= 2 * KU + PRE).astype(jnp.int32)
            drained(r)
            sum_step(r)

        return 0

    lax.fori_loop(0, 2 * KU + 2 * NU + 5, step, 0)

    for p in range(2):
        remote(sc.at[p], sc.at[p], c_send.at[p], c_recv.at[0], partner).wait_send()
        remote(sb.at[p], sb.at[p], b_send.at[p], b_recv.at[0], partner).wait_send()
        remote(sa.at[p], sa.at[p], a_send.at[p], a_recv.at[0], partner).wait_send()
        pltpu.make_async_copy(yst.at[p], y_ref.at[:, pl.ds(0, NW)], y_sem.at[p]).wait()


def fused(meta, x, wg, wu, wd, sg, su, sd):
    vmem = pl.BlockSpec(memory_space=pltpu.VMEM)
    hbm = pl.BlockSpec(memory_space=pl.ANY)
    dma, regular = pltpu.SemaphoreType.DMA, pltpu.SemaphoreType.REGULAR
    return pl.pallas_call(
        kernel,
        out_shape=jax.ShapeDtypeStruct((256, 2560), BF16),
        in_specs=[vmem, vmem] + [hbm] * 6,
        out_specs=hbm,
        scratch_shapes=[
            pltpu.VMEM((16, 16, 256), F32),
            pltpu.VMEM((8, 160, 256), BF16),
            pltpu.VMEM((8, 256, 384), BF16),
            pltpu.VMEM((HB + 3 * NE, 256, KW), BF16),
            pltpu.VMEM((NE, 2, 256, 1536), F32),
            pltpu.VMEM((NE, 256, KW), BF16),
            pltpu.VMEM((2, 2, KW, 1536), BF16),
            pltpu.VMEM((3, 1536, NW), BF16),
            pltpu.VMEM((NU, 256, NW), F32),
            pltpu.VMEM((RING, 8, 320, NW), BF16),
            pltpu.VMEM((NU, 4, 256, NW), BF16),
            pltpu.VMEM((NU, 2, 256, NW), BF16),
            pltpu.VMEM((NU, 256, NW), BF16),
            pltpu.VMEM((2, 4, 256, NW), BF16),
            pltpu.VMEM((2, 2, 256, NW), BF16),
            pltpu.VMEM((2, 256, NW), BF16),
            pltpu.VMEM((2, 256, NW), BF16),
            dma, dma,
            dma((KU,)), dma((KU,)), dma((KU,)), dma((KU,)), dma((KU,)), dma((KU,)),
            regular((KU,)),
            dma((2, 2)), dma((3,)),
            dma((RING,)), dma((RING,)), regular,
            dma((NU,)), dma((NU,)), dma((NU,)), dma((2,)), dma((2,)), dma((2,)), dma((2,)),
        ],
        compiler_params=pltpu.CompilerParams(
            collective_id=0, has_side_effects=True, vmem_limit_bytes=67043328),
        cost_estimate=pl.CostEstimate(flops=67_000_000_000, bytes_accessed=270_000_000, transcendentals=10_000_000),
        name="moe",
    )(meta, x, wg, wu, wd, sg, su, sd)


def solution(mesh):
    def local(x, expert, slot, gate, wg, wu, wd, sg, su, sd):
        x, expert, slot, gate = x[0, 0], expert[0, 0], slot[0, 0], gate[0, 0]
        code = jnp.where(slot < CAP, expert * CAP + slot, -1).astype(F32)
        weight = gate.astype(BF16).astype(F32)
        meta = jnp.concatenate([code, weight], axis=1).T
        return fused(meta, x, wg, wu, wd, sg, su, sd)[None, None]

    tok = P("dp", "ep", None, None)
    wts = P("ep", None, None)
    return jax.shard_map(
        local, mesh=mesh,
        in_specs=(tok, tok, tok, tok, wts, wts, wts, P(None, None), P(None, None), P(None, None)),
        out_specs=tok, check_vma=False)
```

time: 487 us -> 230 us (0.47)
  the two profiles are of different devices: /device:TPU:0 before, /device:TPU:1 now
where the time goes in v1:
time: 230 us; the launch traced here: 229 us
  Pallas kernels  225 us (98%)
  local copies, waits for them, and re-layouts  2.46 us (1%)
    pallas_call x1, Pallas kernels, fused(): pl.pallas_call(kernel, out_shape=jax.ShapeDtypeStruct((256, 2560), BF16),...  225 us

profile of v1, /device:TPU:1, one launch (start us, length us, event | category | flops | bytes accessed | tf_op | source)
XLA Modules:
  0.0 229.3 jit_solution(8602497429272886072)
XLA Ops:
  0.0 0.7 convert_bitcast_fusion
  0.7 0.7 bitcast_convert_fusion
  1.4 0.6 maximum_bitcast_fusion.meta_ref
  2.0 224.8 %moe.1 = bf16[256,2560]{1,0:T(8,128)(2,1)} custom-call(f32[16,256]{1,0:T(8,128)} %maximum_bitcast_fusion.meta_ref, bf16[256,2560]{1,0:T(8,128)(2,1)} %bitcast.10, bf16[5,2560,1536]{2,1,0:T(8,128)(2,1)} %wg_ref.1, bf16[5,2560,1536]{2,1,0:T(8,128)(2,1)} %wu_ref.1, bf16[5,1536,2560]{2,1,0:T(8,128)(2,1)} %wd_ref.1, bf16[2560,1536]{1,0:T(8,128)(2,1)} %sg_ref.1, ...), custom_call_target="tpu_custom_call" | custom-call | flops 67000000512 | bytes 270000000 | tf_op jit(solution)/shard_map/moe/pallas_call | solution.py:475
  226.8 2.5 %copy.12 = bf16[1,1,256,2560]{3,2,1,0:T(8,128)(2,1)} copy(bf16[1,1,256,2560]{3,2,1,0:T(8,128)(2,1)} %bitcast.9) | data formatting | bytes 2621440

commit v2 on v1

--- a/solution.py
+++ b/solution.py
@@ -14,14 +14,16 @@
 NU, NW = 10, 256
 NE, CAP = 5, 32
 RING = 5
-PRE = 4
+LAG = 2, 3, 4
+AHEAD = 3
+DEEP = 5
 HB = 40
 
 
 def kernel(meta_ref, x_ref, wg_ref, wu_ref, wd_ref, sg_ref, su_ref, sd_ref, y_ref,
-           gmeta, onehot, comb, xg, acc, z, wgu, wdn, ys, ob, rc, rb, ra, sc, sb, sa, yst,
+           gmeta, onehot, comb, xg, acc, z, wgu, wdn, ys, ob, hb, rc, rb, ra, sc, sb, sa, yst,
            m_send, m_recv, ag_a, ag_b, ag_c, ag_p, ag_s, ag_ps, free,
-           gu_sem, dn_sem, o_recv, o_send, o_free, c_recv, b_recv, a_recv, c_send, b_send, a_send, y_sem):
+           gu_sem, dn_sem, x_sem, own_sem, o_recv, o_send, o_free, c_recv, b_recv, a_recv, c_send, b_send, a_send, y_sem):
     me = lax.axis_index("ep")
     core = me % 2
     chip = me // 2
@@ -44,42 +46,40 @@
             src_ref=src, dst_ref=dst, send_sem=send, recv_sem=recv, device_id={"ep": dev}, device_id_type=MESH)
 
     def start_gu(i):
-        slot = i % 2
-
-        @pl.when(i < KU)
-        def _():
-            rows = pl.ds(pl.multiple_of(i * KW, KW), KW)
-            pltpu.make_async_copy(sg_ref.at[rows], wgu.at[slot, 0], gu_sem.at[slot, 0]).start()
-            pltpu.make_async_copy(su_ref.at[rows], wgu.at[slot, 1], gu_sem.at[slot, 1]).start()
-
-        @pl.when(jnp.logical_and(i >= KU, i < KU + 2 * KU * NE))
-        def _():
-            m = (i - KU) % (KU * NE)
-            rows = pl.ds(pl.multiple_of((m // NE) * KW, KW), KW)
-            pltpu.make_async_copy(wg_ref.at[m % NE, rows], wgu.at[slot, 0], gu_sem.at[slot, 0]).start()
-            pltpu.make_async_copy(wu_ref.at[m % NE, rows], wgu.at[slot, 1], gu_sem.at[slot, 1]).start()
+        slot = i % 3
+
+        for j, (shared_ref, routed_ref) in enumerate(((sg_ref, wg_ref), (su_ref, wu_ref))):
+            @pl.when(jnp.logical_and(i < 2 * KU, i % 2 == j))
+            def _():
+                rows = pl.ds(pl.multiple_of((i // 2) * KW, KW), KW)
+                pltpu.make_async_copy(shared_ref.at[rows], wgu.at[slot], gu_sem.at[slot]).start()
+
+            @pl.when(jnp.logical_and(jnp.logical_and(i >= 2 * KU, i < 2 * KU + 4 * KU * NE), i % 2 == j))
+            def _():
+                m = ((i - 2 * KU) // 2) % (KU * NE)
+                rows = pl.ds(pl.multiple_of((m // NE) * KW, KW), KW)
+                pltpu.make_async_copy(routed_ref.at[m % NE, rows], wgu.at[slot], gu_sem.at[slot]).start()
 
     def wait_gu(i):
-        slot = i % 2
-        for j in range(2):
-            pltpu.make_async_copy(sg_ref.at[pl.ds(0, KW)], wgu.at[slot, j], gu_sem.at[slot, j]).wait()
+        slot = i % 3
+        pltpu.make_async_copy(sg_ref.at[pl.ds(0, KW)], wgu.at[slot], gu_sem.at[slot]).wait()
 
     def start_dn(i):
-        slot = i % 3
+        slot = i % DEEP
 
         @pl.when(i < NU)
         def _():
             cols = pl.ds(pl.multiple_of(i * NW, NW), NW)
             pltpu.make_async_copy(sd_ref.at[:, cols], wdn.at[slot], dn_sem.at[slot]).start()
 
-        @pl.when(jnp.logical_and(i >= NU, i < NU + 2 * NU * NE))
+        @pl.when(jnp.logical_and(i >= NU, i < NU + NU * NE))
         def _():
             m = i - NU
             cols = pl.ds(pl.multiple_of(((m // NE) % NU) * NW, NW), NW)
             pltpu.make_async_copy(wd_ref.at[m % NE, :, cols], wdn.at[slot], dn_sem.at[slot]).start()
 
     def wait_dn(i):
-        slot = i % 3
+        slot = i % DEEP
         pltpu.make_async_copy(sd_ref.at[:, pl.ds(0, NW)], wdn.at[slot], dn_sem.at[slot]).wait()
 
     def blk(k, s):
@@ -99,7 +99,7 @@
                 remote(x_ref.at[pl.ds(r0, rn), cols], xg.at[blk(k, chip), pl.ds(r0, rn)],
                        ag_s.at[k], sem.at[k], peer(d)).start()
         remote(x_ref.at[:, cols], xg.at[blk(k, chip)], ag_ps.at[k], ag_p.at[k], partner).start()
-        xg[blk(k, chip)] = x_ref[:, cols]
+        pltpu.make_async_copy(x_ref.at[:, cols], xg.at[blk(k, chip)], own_sem.at[k]).start()
 
     def arrived(sem, k, n):
         remote(xg.at[pl.ds(0, n)], xg.at[pl.ds(0, n)], ag_s.at[k], sem.at[k], partner).wait_recv()
@@ -162,15 +162,17 @@
         lax.fori_loop(0, n * 8, body, 0)
 
     def gate_up(i, lhs, e):
-        wait_gu(i)
-        slot = i % 2
         for j in range(2):
-            acc[e, j] += jnp.dot(lhs, wgu[slot, j], preferred_element_type=F32)
-        start_gu(i + 2)
-
-    for i in range(2):
+            t = 2 * i + j
+            wait_gu(t)
+            acc[e, j] += jnp.dot(lhs, wgu[t % 3], preferred_element_type=F32)
+            start_gu(t + 3)
+
+    for n in range(NU):
+        pltpu.make_async_copy(x_ref.at[:, pl.ds(n * NW, NW)], ob.at[n // 8, n % 8, pl.ds(0, 256)], x_sem.at[n]).start()
+    for i in range(3):
         start_gu(jnp.int32(i))
-    for i in range(3):
+    for i in range(DEEP):
         start_dn(jnp.int32(i))
     barrier = pltpu.get_barrier_semaphore()
 
@@ -179,22 +181,6 @@
         return 0
 
     lax.fori_loop(1, 16, greet, 0)
-    pl.semaphore_wait(barrier, 15)
-
-    @pl.when(core == 0)
-    def _():
-        own(jnp.int32(0))
-
-    def tell(i, _):
-        remote(meta_ref, gmeta.at[me], m_send, m_recv, (me + i) % 16).start()
-        return 0
-
-    lax.fori_loop(1, 16, tell, 0)
-    gmeta[me] = meta_ref[...]
-
-    @pl.when(core == 0)
-    def _():
-        own(jnp.int32(1))
 
     def clear(t, _):
         e, r = t // 8, t % 8
@@ -204,6 +190,23 @@
         return 0
 
     lax.fori_loop(0, NE * 8, clear, 0)
+    pl.semaphore_wait(barrier, 15)
+
+    @pl.when(core == 0)
+    def _():
+        own(jnp.int32(0))
+
+    def tell(i, _):
+        remote(meta_ref, gmeta.at[me], m_send, m_recv, (me + i) % 16).start()
+        return 0
+
+    lax.fori_loop(1, 16, tell, 0)
+    gmeta[me] = meta_ref[...]
+
+    @pl.when(core == 0)
+    def _():
+        for k in range(1, AHEAD):
+            own(jnp.int32(k))
 
     def shared(i, _):
         @pl.when(jnp.logical_and(core == 0, i == 1))
@@ -212,30 +215,32 @@
 
         @pl.when(jnp.logical_and(core == 0, i == 4))
         def _():
-            event_b(jnp.int32(0))
-
-        gate_up(i, x_ref[:, pl.ds(pl.multiple_of(i * KW, KW), KW)], 0)
+            event_a(jnp.int32(1))
+
+        n = 2 * i
+        lhs = jnp.concatenate([ob[n // 8, n % 8, :256], ob[(n + 1) // 8, (n + 1) % 8, :256]], axis=1)
+        gate_up(i, lhs, 0)
         return 0
 
+    for n in range(NU):
+        pltpu.make_async_copy(x_ref.at[:, pl.ds(n * NW, NW)], ob.at[n // 8, n % 8, pl.ds(0, 256)], x_sem.at[n]).wait()
     lax.fori_loop(0, KU, shared, 0)
 
     def store_shared(e, q, rows, v):
-        z[q, rows] = v
+        for h in range(2):
+            n = 2 * q + h
+            sc[n // 4, n % 4, rows] = v[:, h * NW:(h + 1) * NW]
 
     act(1, store_shared)
 
-    def shared_down(i, _):
+    def shared_down(i):
         wait_dn(i)
-        slot = i % 3
-        ys[i] = sum(jnp.dot(z[q], wdn[slot, q * KW:(q + 1) * KW], preferred_element_type=F32) for q in range(3))
-        start_dn(i + 3)
-        return 0
-
-    lax.fori_loop(0, NU, shared_down, 0)
-
-    remote(gmeta.at[pl.ds(0, 15)], gmeta.at[pl.ds(0, 15)], m_send, m_recv, partner).wait()
-
-    def build_comb(s, _):
+        slot = i % DEEP
+        ys[i] = sum(jnp.dot(sc[n // 4, n % 4], wdn[slot, n * NW:(n + 1) * NW], preferred_element_type=F32)
+                    for n in range(6))
+        start_dn(i + DEEP)
+
+    def build_comb(s):
         m = gmeta[2 * s + core]
         row = lax.broadcasted_iota(jnp.int32, (384, 256), 0)
         mine = (me * (NE * CAP)).astype(jnp.int32)
@@ -245,9 +250,12 @@
         for j in range(8):
             t = t + jnp.where(target == m[j:j + 1], m[8 + j:9 + j], 0.0)
         comb[s] = t.T.astype(BF16)
-        return 0
-
-    lax.fori_loop(0, 8, build_comb, 0)
+
+    @pl.when(core == 0)
+    def _():
+        event_b(jnp.int32(0))
+
+    remote(gmeta.at[pl.ds(0, 15)], gmeta.at[pl.ds(0, 15)], m_send, m_recv, partner).wait()
 
     def gather_step(g):
         ph, k = g // KU, g % KU
@@ -256,6 +264,7 @@
         @pl.when(core == ph)
         def _():
             event_c(k)
+            pltpu.make_async_copy(x_ref.at[:, pl.ds(0, KW)], xg.at[blk(k, chip)], own_sem.at[k]).wait()
 
         @pl.when(core != ph)
         def _():
@@ -263,7 +272,15 @@
 
         @pl.when(jnp.logical_and(nxt < 2 * KU, core == nxt // KU))
         def _():
-            event_a(nxt % KU)
+            event_b(nxt % KU)
+
+        @pl.when(jnp.logical_and(g + 2 < 2 * KU, core == (g + 2) // KU))
+        def _():
+            event_a((g + 2) % KU)
+
+        @pl.when(jnp.logical_and(g + AHEAD < KU, core == 0))
+        def _():
+            own(g + AHEAD)
 
         @pl.when(k == 0)
         def _():
@@ -286,19 +303,25 @@
         def expert(e, _):
             @pl.when(e == 2)
             def _():
-                @pl.when(jnp.logical_and(nxt < 2 * KU, core == nxt // KU))
+                @pl.when(jnp.logical_and(jnp.logical_and(g >= 2, g <= 6), core == 1))
                 def _():
-                    event_b(nxt % KU)
-
-                @pl.when(jnp.logical_and(g + 2 < 2 * KU, core == (g + 2) // KU))
-                def _():
-                    own(g + 2)
+                    own(g + 3)
 
             gate_up(KU + g * NE + e, z[e], e)
             return 0
 
         lax.fori_loop(0, NE, expert, 0)
 
+        @pl.when(g < NU // 2)
+        def _():
+            shared_down(2 * g)
+            shared_down(2 * g + 1)
+
+        @pl.when(g < 4)
+        def _():
+            build_comb(2 * g)
+            build_comb(2 * g + 1)
+
         @pl.when(jnp.logical_and(ph == 0, core == 0))
         def _():
             sent(k)
@@ -326,13 +349,13 @@
 
     def sum_step(r):
         def main(v):
-            return jnp.logical_and(jnp.logical_and(v >= 0, v < 2 * NU), core == v // NU)
-
-        v4 = r - 5
+            return jnp.logical_and(v >= 0, v < NU)
+
+        v4 = r - LAG[2]
 
         @pl.when(main(v4))
         def _():
-            u, slot, p = v4 % NU, v4 % RING, v4 % 2
+            u, slot, p = v4, v4 % RING, v4 % 2
             remote(ra.at[u], ra.at[u], a_send.at[0], a_recv.at[u], partner).wait_recv()
             val = term(slot, chip, 0, 256) + rc[u, 0].astype(F32) + rb[u, 0].astype(F32) + ra[u].astype(F32) + ys[u]
 
@@ -348,11 +371,11 @@
             def _():
                 pl.semaphore_signal(o_free, inc=1, device_id={"ep": partner}, device_id_type=MESH)
 
-        v3 = r - 4
+        v3 = r - LAG[1]
 
         @pl.when(main(v3))
         def _():
-            u, slot, p = v3 % NU, v3 % RING, v3 % 2
+            u, slot, p = v3, v3 % RING, v3 % 2
             remote(rb.at[u], rb.at[u], b_send.at[0], b_recv.at[u], partner).wait_recv()
 
             @pl.when(u >= 2)
@@ -368,11 +391,11 @@
                 a, b, c = order(i, u)
                 remote(sa.at[p, pl.ds(r0, rn)], ra.at[u, pl.ds(r0, rn)], a_send.at[p], a_recv.at[u], peer(a)).start()
 
-        v2 = r - 3
+        v2 = r - LAG[0]
 
         @pl.when(main(v2))
         def _():
-            u, slot, p = v2 % NU, v2 % RING, v2 % 2
+            u, slot, p = v2, v2 % RING, v2 % 2
             remote(rc.at[u], rc.at[u], c_send.at[0], c_recv.at[u], partner).wait_recv()
 
             @pl.when(u >= 2)
@@ -390,37 +413,42 @@
                 remote(sb.at[p, :, pl.ds(r0, rn)], rb.at[u, :, pl.ds(r0, rn)], b_send.at[p], b_recv.at[u],
                        peer(b)).start()
 
-        @pl.when(r < 2 * NU)
-        def _():
-            ph, slot = r // NU, r % RING
+        @pl.when(r < NU)
+        def _():
+            slot, p = r % RING, r % 2
+            there = hb.at[p], ob.at[slot, :, pl.ds(160, 160)], o_send.at[p], o_recv.at[slot], partner
+
+            @pl.when(r >= 2)
+            def _():
+                remote(*there).wait_send()
 
             for e in range(NE):
                 i = NU + r * NE + e
                 wait_dn(i)
-                o = sum(jnp.dot(xg[HB * (1 - ph) + e * 3 + q], wdn[i % 3, q * KW:(q + 1) * KW],
+                own_o, other_o = (
+                    sum(jnp.dot(xg[base + e * 3 + q], wdn[i % DEEP, q * KW:(q + 1) * KW],
                                 preferred_element_type=F32) for q in range(3)).astype(BF16)
+                    for base in (HB * (1 - core), HB * core))
                 for s in range(8):
-                    ob[slot, s, e * CAP:(e + 1) * CAP] = o[s * CAP:(s + 1) * CAP]
-                start_dn(i + 3)
-
-            @pl.when(core != ph)
-            def _():
-                @pl.when(r % NU >= RING)
-                def _():
-                    pl.semaphore_wait(o_free, 1)
-
-                remote(ob.at[slot, :, pl.ds(0, 160)], ob.at[slot, :, pl.ds(160, 160)], o_send.at[slot],
-                       o_recv.at[slot], partner).start()
-
-        v1 = r - 1
+                    ob[slot, s, e * CAP:(e + 1) * CAP] = own_o[s * CAP:(s + 1) * CAP]
+                    hb[p, s, e * CAP:(e + 1) * CAP] = other_o[s * CAP:(s + 1) * CAP]
+                start_dn(i + DEEP)
+
+            @pl.when(r >= RING)
+            def _():
+                pl.semaphore_wait(o_free, 1)
+
+            remote(*there).start()
+
+        v1 = r
 
         @pl.when(main(v1))
         def _():
-            u, slot, p = v1 % NU, v1 % RING, v1 % 2
+            u, slot, p = v1, v1 % RING, v1 % 3
             part = ob.at[slot, :, pl.ds(160, 160)]
             remote(part, part, o_send.at[slot], o_recv.at[slot], partner).wait_recv()
 
-            @pl.when(u >= 2)
+            @pl.when(u >= 3)
             def _():
                 remote(sc.at[p], sc.at[p], c_send.at[p], c_recv.at[0], partner).wait_send()
 
@@ -435,34 +463,24 @@
                 remote(sc.at[p, :, pl.ds(r0, rn)], rc.at[u, :, pl.ds(r0, rn)], c_send.at[p], c_recv.at[u],
                        peer(c)).start()
 
-    def drained(r):
-        v = r - RING
-
-        @pl.when(jnp.logical_and(v >= 0, core != v // NU))
-        def _():
-            slot = v % RING
-            part = ob.at[slot, :, pl.ds(0, 160)]
-            remote(part, part, o_send.at[slot], o_recv.at[slot], partner).wait_send()
-
     def step(m, _):
-        gather = jnp.logical_or(m < 2 * KU - 1, m == 2 * KU - 1 + PRE)
-
-        @pl.when(gather)
-        def _():
-            gather_step(m - PRE * (m // (2 * KU - 1)))
-
-        @pl.when(jnp.logical_not(gather))
-        def _():
-            r = m - (2 * KU - 1) - (m >= 2 * KU + PRE).astype(jnp.int32)
-            drained(r)
-            sum_step(r)
+        @pl.when(m < 2 * KU)
+        def _():
+            gather_step(m)
+
+        @pl.when(m >= 2 * KU)
+        def _():
+            sum_step(m - 2 * KU)
 
         return 0
 
-    lax.fori_loop(0, 2 * KU + 2 * NU + 5, step, 0)
-
+    lax.fori_loop(0, 2 * KU + NU + LAG[2], step, 0)
+
+    for p in range(3):
+        remote(sc.at[p], sc.at[p], c_send.at[p], c_recv.at[0], partner).wait_send()
     for p in range(2):
-        remote(sc.at[p], sc.at[p], c_send.at[p], c_recv.at[0], partner).wait_send()
+        part = ob.at[0, :, pl.ds(160, 160)]
+        remote(hb.at[p], part, o_send.at[p], o_recv.at[0], partner).wait_send()
         remote(sb.at[p], sb.at[p], b_send.at[p], b_recv.at[0], partner).wait_send()
         remote(sa.at[p], sa.at[p], a_send.at[p], a_recv.at[0], partner).wait_send()
         pltpu.make_async_copy(yst.at[p], y_ref.at[:, pl.ds(0, NW)], y_sem.at[p]).wait()
@@ -475,7 +493,7 @@
     return pl.pallas_call(
         kernel,
         out_shape=jax.ShapeDtypeStruct((256, 2560), BF16),
-        in_specs=[vmem, vmem] + [hbm] * 6,
+        in_specs=[vmem] + [hbm] * 7,
         out_specs=hbm,
         scratch_shapes=[
             pltpu.VMEM((16, 16, 256), F32),
@@ -484,23 +502,24 @@
             pltpu.VMEM((HB + 3 * NE, 256, KW), BF16),
             pltpu.VMEM((NE, 2, 256, 1536), F32),
             pltpu.VMEM((NE, 256, KW), BF16),
-            pltpu.VMEM((2, 2, KW, 1536), BF16),
-            pltpu.VMEM((3, 1536, NW), BF16),
+            pltpu.VMEM((3, KW, 1536), BF16),
+            pltpu.VMEM((DEEP, 1536, NW), BF16),
             pltpu.VMEM((NU, 256, NW), F32),
             pltpu.VMEM((RING, 8, 320, NW), BF16),
+            pltpu.VMEM((2, 8, 160, NW), BF16),
             pltpu.VMEM((NU, 4, 256, NW), BF16),
             pltpu.VMEM((NU, 2, 256, NW), BF16),
             pltpu.VMEM((NU, 256, NW), BF16),
-            pltpu.VMEM((2, 4, 256, NW), BF16),
+            pltpu.VMEM((3, 4, 256, NW), BF16),
             pltpu.VMEM((2, 2, 256, NW), BF16),
             pltpu.VMEM((2, 256, NW), BF16),
             pltpu.VMEM((2, 256, NW), BF16),
             dma, dma,
             dma((KU,)), dma((KU,)), dma((KU,)), dma((KU,)), dma((KU,)), dma((KU,)),
             regular((KU,)),
-            dma((2, 2)), dma((3,)),
-            dma((RING,)), dma((RING,)), regular,
-            dma((NU,)), dma((NU,)), dma((NU,)), dma((2,)), dma((2,)), dma((2,)), dma((2,)),
+            dma((3,)), dma((DEEP,)), dma((NU,)), dma((KU,)),
+            dma((RING,)), dma((2,)), regular,
+            dma((NU,)), dma((NU,)), dma((NU,)), dma((3,)), dma((2,)), dma((2,)), dma((2,)),
         ],
         compiler_params=pltpu.CompilerParams(
             collective_id=0, has_side_effects=True, vmem_limit_bytes=67043328),

time: 230 us -> 209 us (0.909)
  the two profiles are of different devices: /device:TPU:1 before, /device:TPU:0 now
where the time goes in v2:
time: 209 us
  Pallas kernels  204 us (98%)
  local copies, waits for them, and re-layouts  2.46 us (1%)
    pallas_call x1, Pallas kernels, fused(): pl.pallas_call(kernel, out_shape=jax.ShapeDtypeStruct((256, 2560), BF16),...  204 us

profile of v2, /device:TPU:0, one launch (start us, length us, event | category | flops | bytes accessed | tf_op | source)
XLA Modules:
  0.0 209.0 jit_solution(11469626686930087545)
XLA Ops:
  0.0 0.7 convert_bitcast_fusion
  0.7 0.7 bitcast_convert_fusion
  1.4 0.6 maximum_bitcast_fusion.meta_ref
  2.0 204.5 %moe.1 = bf16[256,2560]{1,0:T(8,128)(2,1)} custom-call(f32[16,256]{1,0:T(8,128)} %maximum_bitcast_fusion.meta_ref, bf16[256,2560]{1,0:T(8,128)(2,1)} %bitcast.10, bf16[5,2560,1536]{2,1,0:T(8,128)(2,1)} %wg_ref.1, bf16[5,2560,1536]{2,1,0:T(8,128)(2,1)} %wu_ref.1, bf16[5,1536,2560]{2,1,0:T(8,128)(2,1)} %wd_ref.1, bf16[2560,1536]{1,0:T(8,128)(2,1)} %sg_ref.1, ...), custom_call_target="tpu_custom_call" | custom-call | flops 67000000512 | bytes 270000000 | tf_op jit(solution)/shard_map/moe/pallas_call | solution.py:493
  206.5 2.5 %copy.12 = bf16[1,1,256,2560]{3,2,1,0:T(8,128)(2,1)} copy(bf16[1,1,256,2560]{3,2,1,0:T(8,128)(2,1)} %bitcast.9) | data formatting | bytes 2621440

commit v3 on v2

--- a/solution.py
+++ b/solution.py
@@ -14,7 +14,7 @@
 NU, NW = 10, 256
 NE, CAP = 5, 32
 RING = 5
-LAG = 2, 3, 4
+LAG = 3, 4, 5
 AHEAD = 3
 DEEP = 5
 HB = 40
@@ -440,7 +440,7 @@
 
             remote(*there).start()
 
-        v1 = r
+        v1 = r - 1
 
         @pl.when(main(v1))
         def _():

time: 209 us -> 203 us (0.971)
  Pallas kernels: 204 us -> 198 us
    pallas_call x1, Pallas kernels: 204 us -> 198 us  [fused(): pl.pallas_call(kernel, out_shape=jax.ShapeDtypeStruct((256, 2560), BF16),...]
where the time goes in v3:
time: 203 us; the launch traced here: 202 us
  Pallas kernels  198 us (98%)
  local copies, waits for them, and re-layouts  2.46 us (1%)
    pallas_call x1, Pallas kernels, fused(): pl.pallas_call(kernel, out_shape=jax.ShapeDtypeStruct((256, 2560), BF16),...  198 us

profile of v3, /device:TPU:0, one launch (start us, length us, event | category | flops | bytes accessed | tf_op | source)
XLA Modules:
  0.0 202.3 jit_solution(5977627904211425784)
XLA Ops:
  0.0 0.7 convert_bitcast_fusion
  0.7 0.7 bitcast_convert_fusion
  1.4 0.6 maximum_bitcast_fusion.meta_ref
  2.0 197.8 %moe.1 = bf16[256,2560]{1,0:T(8,128)(2,1)} custom-call(f32[16,256]{1,0:T(8,128)} %maximum_bitcast_fusion.meta_ref, bf16[256,2560]{1,0:T(8,128)(2,1)} %bitcast.10, bf16[5,2560,1536]{2,1,0:T(8,128)(2,1)} %wg_ref.1, bf16[5,2560,1536]{2,1,0:T(8,128)(2,1)} %wu_ref.1, bf16[5,1536,2560]{2,1,0:T(8,128)(2,1)} %wd_ref.1, bf16[2560,1536]{1,0:T(8,128)(2,1)} %sg_ref.1, ...), custom_call_target="tpu_custom_call" | custom-call | flops 67000000512 | bytes 270000000 | tf_op jit(solution)/shard_map/moe/pallas_call | solution.py:493
  199.9 2.5 %copy.12 = bf16[1,1,256,2560]{3,2,1,0:T(8,128)(2,1)} copy(bf16[1,1,256,2560]{3,2,1,0:T(8,128)(2,1)} %bitcast.9) | data formatting | bytes 2621440
